TPU v7x, 32 devices: a whole 2x2x4 slice. The times are simulated.
32 devices in a mesh: gossip: 16 (over z, y, core), mp: 2 (over x).
Axes of the slice: x: 2, y: 2, z: 4, core: 2. Of those that a mesh axis runs over, the one named last changes fastest.
Arguments:
- params: float32 [16, 1024, 4096], P('gossip', None, 'mp'), may hold values from -6 to 6
- public: float32 [16, 1024, 64], P('gossip'), may hold values from -12 to 12
- gradients: bfloat16 [2, 16, 1024, 4096], P(None, 'gossip', None, 'mp'), may hold values from -130 to 130
- projection: float32 [4096, 64], P('mp'), may hold values from -0.09375 to 0.09375
- partners: int32 [2, 16], P(None, 'gossip'), may hold values from 0 to 15, as said below
Outputs:
- params_out: float32 [16, 1024, 4096], P('gossip', None, 'mp')
- public_out: float32 [16, 1024, 64], P('gossip')
- consensus: float32 [2], replicated
- grad_norm: float32 [2], replicated
Inputs may be any that keep to these rules, and one draw needn't show every extreme that they name: Each row is a pairing of the 16 replicas: partners[r, partners[r, i]] = i and partners[r, i] != i.
All inputs are finite; a program needn't handle non-finite values.
Results may differ from a plain program's by a relative error of at most 0.008.
Values may be sent and summed in bfloat16 or wider, within the bound.
A program may use at most 64 MiB of HBM per device.

v0:
```python
import functools

import jax
import jax.numpy as jnp
from jax import lax
from jax.experimental import pallas as pl
from jax.experimental.pallas import tpu as pltpu
from jax.sharding import PartitionSpec as P

ROUNDS = 2
step_size = 1.0
clip_limit = 0.5
mixing = 0.4
epsilon = 1e-06

F32 = jnp.float32
BF16 = jnp.bfloat16
HIGHEST = lax.Precision.HIGHEST
VMEM = pl.BlockSpec(memory_space=pltpu.VMEM)
SMEM = pl.BlockSpec(memory_space=pltpu.SMEM)


def high_low(value):
    high = value.astype(BF16)
    return high, (value - high.astype(F32)).astype(BF16)


def dot(a, b):
    return jnp.dot(a, b, preferred_element_type=F32)


def dot_t(a, b):
    return lax.dot_general(a, b, (((1,), (1,)), ((), ())), preferred_element_type=F32)


def exchange(groups, members, total, w_hbm, g_hbm, c_ref, p_ref, partners_ref, half_hbm, f_ref, stat_ref,
             wv, gv, basis, squares, a_ref, b_ref, d_ref,
             tiles, tiles_mp, grams, local, arrived, owned, first, reply, second, final, cons, cons_mp,
             send_g, recv_g, send_m, recv_m, send_u, recv_u, send_f, recv_f, load_g, load_w, store_w):
    g = lax.axis_index("gossip")
    m = lax.axis_index("mp")
    rows = owned.shape[1]
    lanes = owned.shape[2]
    rank = lanes // 2
    flat = groups * rows
    height, columns = wv.shape
    steps = load_w.shape[0]
    chunk = height // steps

    def span(i):
        return pl.ds(pl.multiple_of(i * chunk, chunk), chunk)

    def each(low, high, act):
        lax.fori_loop(low, high, lambda i, _: (act(i), 0)[1], 0)

    def grad_copy(i):
        return pltpu.make_async_copy(g_hbm.at[:, 0, span(i)], gv.at[:, span(i)], load_g.at[i])

    def weight_copy(i):
        return pltpu.make_async_copy(w_hbm.at[0, span(i)], wv.at[span(i)], load_w.at[i])

    def half_copy(i):
        return pltpu.make_async_copy(wv.at[span(i)], half_hbm.at[0, span(i)], store_w.at[i])

    each(0, steps, lambda i: grad_copy(i).start())
    each(0, steps, lambda i: weight_copy(i).start())

    def peers(count, here, act):
        each(1, count, lambda k: act(lax.rem(here + k, count)))

    barrier = pltpu.get_barrier_semaphore()

    def greet(axis):
        def act(peer):
            pl.semaphore_signal(barrier, inc=1, device_id={axis: peer}, device_id_type=pl.DeviceIdType.MESH)
        return act

    peers(groups, g, greet("gossip"))
    peers(members, m, greet("mp"))

    def copy(axis, slot, src, dst, peer, into):
        send, recv = (send_g, recv_g) if axis == "gossip" else (send_m, recv_m)
        return pltpu.make_async_remote_copy(
            src_ref=src, dst_ref=dst, send_sem=send.at[slot, peer], recv_sem=recv.at[slot, into],
            device_id={axis: peer}, device_id_type=pl.DeviceIdType.MESH)

    def start(axis, slot, source, target):
        count, here = (groups, g) if axis == "gossip" else (members, m)
        peers(count, here, lambda p: copy(axis, slot, source(p), target.at[here], p, here).start())

    def finish(axis, slot, source, target):
        count, here = (groups, g) if axis == "gossip" else (members, m)
        peers(count, here, lambda p: copy(axis, slot, source(p), target.at[p], p, p).wait())

    def part_copy(p, q, into):
        return pltpu.make_async_remote_copy(
            src_ref=local.at[q, p], dst_ref=arrived.at[into, p], send_sem=send_u.at[p, q], recv_sem=recv_u.at[p, into],
            device_id={"mp": q}, device_id_type=pl.DeviceIdType.MESH)

    def result_copy(p, q, into):
        return pltpu.make_async_remote_copy(
            src_ref=second.at[p], dst_ref=final.at[into, p], send_sem=send_f.at[p, q], recv_sem=recv_f.at[p, into],
            device_id={"mp": q}, device_id_type=pl.DeviceIdType.MESH)

    high, low = high_low(p_ref[...])
    basis[...] = jnp.concatenate([high, low], axis=0)
    parts = dot_t(basis[...], basis[...])
    folded = parts + pltpu.roll(parts, rank, 1)
    gram = folded[:rank] + folded[rank:]
    gram_row = lax.broadcasted_iota(jnp.int32, gram.shape, 0)
    gram_col = lax.broadcasted_iota(jnp.int32, gram.shape, 1)
    gram = jnp.where(gram_col < rank, gram, 0.0)
    mixer = jnp.where(gram_row == gram_col, 1.0 / members, 0.0) - gram
    a_ref[...] = lax.dot_general(c_ref[...], mixer, (((0,), (0,)), ((), ())), precision=HIGHEST,
                                 preferred_element_type=F32)
    squares[...] = jnp.zeros_like(squares)
    grams[m] = gram

    def fold(value):
        return value + pltpu.roll(value, rank, 1)

    def grad_step(i):
        grad_copy(i).wait()
        for index in range(ROUNDS):
            grad = gv[index, span(i)]
            wide = grad.astype(F32)
            squares[index] += jnp.sum((wide * wide).reshape(chunk // 8, 8, columns), axis=0)
            product = fold(dot_t(grad, basis[...]))
            if index == 0:
                b_ref[span(i)] = product
            else:
                lane = lax.broadcasted_iota(jnp.int32, product.shape, 1)
                d_ref[span(i)] = jnp.where(lane < rank, 0.0, product)

    def weight_step(i):
        weight_copy(i).wait()
        high, low = high_low(wv[span(i)])
        a_ref[span(i)] += fold(dot_t(high, basis[...]) + dot_t(low, basis[...]))

    each(0, steps, grad_step)
    row = lax.broadcasted_iota(jnp.int32, (8, 128), 0)
    tile = jnp.where(row == 0, jnp.sum(squares[0]), jnp.sum(squares[1]))
    tile = jnp.where(row == 2, partners_ref[0].astype(F32), tile)
    tile = jnp.where(row == 3, partners_ref[1].astype(F32), tile)
    tiles[g] = tile
    pl.semaphore_wait(barrier, groups - 1 + members - 1)

    start("gossip", 0, lambda p: tiles.at[g], tiles)
    start("mp", 0, lambda p: grams.at[m], grams)
    each(0, steps // 2, weight_step)
    finish("gossip", 0, lambda p: tiles.at[g], tiles)
    tiles_mp[m] = jnp.sum(tiles[...], axis=0)
    start("mp", 1, lambda p: tiles_mp.at[m], tiles_mp)
    each(steps // 2, steps, weight_step)
    finish("mp", 1, lambda p: tiles_mp.at[m], tiles_mp)
    norm = jnp.sqrt(jnp.sum(tiles_mp[...], axis=0) / total + epsilon)
    scale = step_size * jnp.minimum(1.0, clip_limit / norm)

    local[...] = (a_ref[...] - scale[0:1, :] * b_ref[...] - scale[1:2, :] * d_ref[...]).reshape(local.shape)
    each(1, groups + 1, lambda k: peers(members, m, lambda q: part_copy(lax.rem(g + k, groups), q, m).start()))
    lane = lax.broadcasted_iota(jnp.int32, (rows, lanes), 1)

    def take(p):
        peers(members, m, lambda q: part_copy(p, q, q).wait_recv())
        summed = local[m, p]
        for index in range(1, members):
            summed = summed + arrived[lax.rem(m + index, members), p]
        return jnp.where(lane < rank, summed.astype(BF16).astype(F32), summed)

    def pass_on(p):
        owned[p] = take(p)
        copy("gossip", 1, owned.at[p], first.at[g], p, g).start()

    peers(groups, g, pass_on)
    first[g] = take(g)

    def half_step(i):
        wide = [gv[index, span(i)].astype(F32) for index in range(ROUNDS)]
        wv[span(i)] = wv[span(i)] - scale[0, 0] * wide[0] - scale[1, 0] * wide[1]
        half_copy(i).start()

    each(0, steps, half_step)

    finish("mp", 0, lambda p: grams.at[m], grams)
    gram = jnp.sum(grams[...], axis=0)[:, :rank]
    inside = lax.broadcasted_iota(jnp.int32, (rows, flat), 0).astype(F32)
    column = lax.broadcasted_iota(jnp.int32, (rows, flat), 1).astype(F32)
    choose = []
    for index in range(ROUNDS):
        blocks = []
        for replica in range(groups):
            wanted = tiles[replica, 2 + index : 3 + index, 0:1] * float(rows) + inside
            blocks.append(jnp.where(wanted == column, 1.0, 0.0))
        choose.append(jnp.concatenate(blocks, axis=0).astype(BF16))
    finish("gossip", 1, lambda p: owned.at[p], first)

    def through(value):
        return jnp.dot(value, gram, precision=HIGHEST, preferred_element_type=F32)

    state = first[...].reshape(flat, lanes)
    sent = state[:, :rank]
    apart = dot(choose[0], sent.astype(BF16)) - sent
    seen = through(apart)
    spread = [jnp.sum(apart * seen)]
    again = (state[:, rank:] + sent + mixing * seen - through(sent)).astype(BF16)
    sent = again.astype(F32)
    later = dot(choose[1], again) - sent
    spread.append(jnp.sum(later * through(later)))
    answer = jnp.concatenate([mixing * (apart + later), sent], axis=1)
    reply[...] = answer.reshape(groups, rows, lanes)
    cons[g] = jnp.where(row == 0, spread[0], spread[1])
    start("gossip", 2, lambda p: reply.at[p], second)
    start("gossip", 3, lambda p: cons.at[g], cons)
    second[g] = reply[g]
    final[m, g] = reply[g]
    peers(members, m, lambda q: result_copy(g, q, m).start())

    def hand_over(p):
        copy("gossip", 2, reply.at[p], second.at[p], p, p).wait()
        final[m, p] = second[p]
        peers(members, m, lambda q: result_copy(p, q, m).start())

    peers(groups, g, hand_over)
    finish("gossip", 3, lambda p: cons.at[g], cons)
    cons_mp[m] = jnp.sum(cons[...], axis=0)
    start("mp", 4, lambda p: cons_mp.at[m], cons_mp)
    each(0, steps, lambda i: half_copy(i).wait())
    each(0, groups, lambda p: peers(members, m, lambda q: part_copy(p, q, q).wait_send()))
    each(0, groups, lambda p: peers(members, m, lambda q: result_copy(p, q, q).wait()))
    finish("mp", 4, lambda p: cons_mp.at[m], cons_mp)
    f_ref[...] = final[...]
    drift = jnp.sum(cons_mp[...], axis=0) / total
    stat_ref[0] = norm
    stat_ref[1] = scale
    stat_ref[2] = drift


def blend(h_ref, f_ref, p_ref, stat_ref, out_ref, c_ref, drift_ref, norm_ref, basis):
    rank = p_ref.shape[0]

    @pl.when(pl.program_id(0) == 0)
    def _():
        high, low = high_low(p_ref[...])
        basis[...] = jnp.concatenate([high, high, low], axis=0)
        for index in range(ROUNDS):
            norm_ref[index] = jnp.max(stat_ref[0, index : index + 1, :])
            drift_ref[index] = jnp.max(stat_ref[2, index : index + 1, :])

    high, low = high_low(f_ref[:, :rank])
    out_ref[0] = h_ref[0] + dot(jnp.concatenate([high, low, high], axis=1), basis[...])
    c_ref[...] = f_ref[...].T[rank:]


def body(params, public, gradients, projection, partners):
    groups = lax.axis_size("gossip")
    members = lax.axis_size("mp")
    _, height, columns = params.shape
    rank = projection.shape[1]
    lanes = 2 * rank
    total = groups * height * columns * members
    tile = min(128, height)
    steps = height // tile
    rows = height // (groups * members)
    split = (members, groups, rows, lanes)
    pieces = (groups, rows, lanes)
    basis = projection.T
    anywhere = pl.BlockSpec(memory_space=pl.ANY)
    dma = pltpu.SemaphoreType.DMA
    half, final, stats = pl.pallas_call(
        functools.partial(exchange, groups, members, total),
        in_specs=[anywhere, anywhere, VMEM, VMEM, SMEM],
        out_specs=[anywhere, VMEM, VMEM],
        out_shape=[jax.ShapeDtypeStruct(params.shape, F32), jax.ShapeDtypeStruct(split, F32),
                   jax.ShapeDtypeStruct((3, 8, 128), F32)],
        scratch_shapes=[
            pltpu.VMEM((height, columns), F32),
            pltpu.VMEM((ROUNDS, height, columns), BF16),
            pltpu.VMEM((lanes, columns), BF16),
            pltpu.VMEM((ROUNDS, 8, columns), F32),
            pltpu.VMEM((height, lanes), F32),
            pltpu.VMEM((height, lanes), F32),
            pltpu.VMEM((height, lanes), F32),
            pltpu.VMEM((groups, 8, 128), F32),
            pltpu.VMEM((members, 8, 128), F32),
            pltpu.VMEM((members, rank, lanes), F32),
            pltpu.VMEM(split, F32),
            pltpu.VMEM(split, F32),
            pltpu.VMEM(pieces, F32),
            pltpu.VMEM(pieces, F32),
            pltpu.VMEM(pieces, F32),
            pltpu.VMEM(pieces, F32),
            pltpu.VMEM(split, F32),
            pltpu.VMEM((groups, 8, 128), F32),
            pltpu.VMEM((members, 8, 128), F32),
            dma((4, groups)), dma((4, groups)), dma((5, members)), dma((5, members)),
            dma((groups, members)), dma((groups, members)), dma((groups, members)), dma((groups, members)),
            dma((steps,)), dma((steps,)), dma((steps,)),
        ],
        compiler_params=pltpu.CompilerParams(collective_id=0, has_side_effects=True),
        name="exchange",
    )(params, gradients, public[0].T, basis, partners.reshape(ROUNDS))

    w_spec = pl.BlockSpec((1, tile, columns), lambda i: (0, i, 0))
    weights, coefs, drift, norm = pl.pallas_call(
        blend,
        grid=(steps,),
        in_specs=[w_spec, pl.BlockSpec((tile, lanes), lambda i: (i, 0)),
                  pl.BlockSpec((rank, columns), lambda i: (0, 0)), VMEM],
        out_specs=[w_spec, pl.BlockSpec((rank, tile), lambda i: (0, i)), SMEM, SMEM],
        out_shape=[jax.ShapeDtypeStruct(params.shape, F32), jax.ShapeDtypeStruct((rank, height), F32),
                   jax.ShapeDtypeStruct((ROUNDS,), F32), jax.ShapeDtypeStruct((ROUNDS,), F32)],
        scratch_shapes=[pltpu.VMEM((3 * rank, columns), BF16)],
        compiler_params=pltpu.CompilerParams(dimension_semantics=("arbitrary",)),
        name="blend",
    )(half, final.reshape(height, lanes), basis, stats)
    return (weights, coefs.T[None], drift, norm)


def solution(mesh):
    return jax.shard_map(
        body,
        mesh=mesh,
        in_specs=(
            P("gossip", None, "mp"),
            P("gossip", None, None),
            P(None, "gossip", None, "mp"),
            P("mp", None),
            P(None, "gossip"),
        ),
        out_specs=(P("gossip", None, "mp"), P("gossip", None, None), P(), P()),
        check_vma=False,
    )
```

profile of v0, /device:TPU:14, one launch (start us, length us, event | category | flops | bytes accessed | tf_op | source)
XLA Modules:
  0.0 57.4 jit_solution(3483169803987036083)
XLA Ops:
  0.6 46.4 %exchange.1 = (f32[1,1024,2048]{2,1,0:T(8,128)}, f32[2,16,32,128]{3,2,1,0:T(8,128)}, f32[3,8,128]{2,1,0:T(8,128)}) custom-call(f32[1,1024,2048]{2,1,0:T(8,128)} %w_hbm.1, bf16[2,1,1024,2048]{3,2,1,0:T(8,128)(2,1)} %g_hbm.1, f32[64,1024]{1,0:T(8,128)} %bitcast.12, f32[64,2048]{1,0:T(8,128)} %bitcast.9, s32[2]{0:T(128)} %bitcast.13), custom_call_target="tpu_custom_call" | custom-call | tf_op jit(solution)/shard_map/exchange/pallas_call | solution.py:269
  47.0 10.4 %blend.1 = (f32[1,1024,2048]{2,1,0:T(8,128)}, f32[64,1024]{1,0:T(8,128)}, f32[2]{0:T(128)}, f32[2]{0:T(128)}) custom-call(f32[1,1024,2048]{2,1,0:T(8,128)} %get-tuple-element.11.h_ref, f32[1024,128]{1,0:T(8,128)} %bitcast.11, f32[64,2048]{1,0:T(8,128)} %bitcast.10, f32[3,8,128]{2,1,0:T(8,128)} %get-tuple-element.13.stat_ref), custom_call_target="tpu_custom_call" | custom-call | tf_op jit(solution)/shard_map/blend/pallas_call | solution.py:304
where the time goes:
time: 57.7 us; the launch traced here: 57.4 us
  Pallas kernels  56.8 us (98%)
  between operations  0.64 us (1%)
    pallas_call x1, Pallas kernels, body(): pl.pallas_call(functools.partial(exchange, groups, members, total), in_sp...  46.4 us
    pallas_call x1, Pallas kernels, body(): pl.pallas_call(blend, grid=(steps,), in_specs=[w_spec, pl.BlockSpec((tile...  10.4 us

commit v1 on v0

v1 whole, which is shorter than its diff:
```python
import functools

import jax
import jax.numpy as jnp
from jax import lax
from jax.experimental import pallas as pl
from jax.experimental.pallas import tpu as pltpu
from jax.sharding import PartitionSpec as P

ROUNDS = 2
step_size = 1.0
clip_limit = 0.5
mixing = 0.4
epsilon = 1e-06

F32 = jnp.float32
BF16 = jnp.bfloat16
VMEM = pl.BlockSpec(memory_space=pltpu.VMEM)
HBM = pl.BlockSpec(memory_space=pltpu.HBM)
ANYWHERE = pl.BlockSpec(memory_space=pl.ANY)
MESH = pl.DeviceIdType.MESH


def high_low(value):
    high = value.astype(BF16)
    return high, (value - high.astype(F32)).astype(BF16)


def dot(a, b):
    return jnp.dot(a, b, preferred_element_type=F32)


def dot_t(a, b):
    return lax.dot_general(a, b, (((1,), (1,)), ((), ())), preferred_element_type=F32)


def t_dot(a, b):
    return lax.dot_general(a, b, (((0,), (0,)), ((), ())), preferred_element_type=F32)


def each(low, high, act):
    lax.fori_loop(low, high, lambda i, _: (act(i), 0)[1], 0)


def exchange(groups, members, total, w_hbm, g_hbm, c_hbm, p_hbm, partners_hbm,
             half_ref, f_ref, basis, stat_ref,
             gv, cv, pv, partners_ref, squares, bd_own, a_own, extra, bd_send, bd_in, a_send, a_in, grams,
             norms, pairs, cons, owned, first, choose, apart_ref, reply, final,
             load_g, load_w, load_p, send_n, recv_n, send_t, recv_t, send_m, recv_m,
             send_u, recv_u, send_f, recv_f):
    g = lax.axis_index("gossip")
    m = lax.axis_index("mp")
    count = groups * members
    me = g * members + m
    phases, block, lanes = bd_own.shape
    subs = a_in.shape[2]
    step = block // subs
    steps = phases * members * subs
    rows = owned.shape[2]
    flat = groups * rows
    rank = lanes // 2
    columns = gv.shape[2]

    def span(i):
        j = i // subs
        q = lax.rem(m + j % members + 1, members)
        start = ((j // members) * members + q) * block + (i % subs) * step
        return pl.ds(pl.multiple_of(start, step), step)

    def grad_copy(i):
        return pltpu.make_async_copy(g_hbm.at[:, 0, span(i)], gv.at[:, span(i)], load_g.at[i])

    def weight_copy(i):
        return pltpu.make_async_copy(w_hbm.at[0, span(i)], half_ref.at[0, span(i)], load_w.at[i])

    basis_copy = pltpu.make_async_copy(p_hbm, pv, load_p.at[0])
    public_copy = pltpu.make_async_copy(c_hbm, cv, load_p.at[1])
    partners_copy = pltpu.make_async_copy(partners_hbm, partners_ref, load_p.at[2])
    basis_copy.start()
    partners_copy.start()
    each(0, steps, lambda i: grad_copy(i).start())

    def device(k):
        d = lax.rem(me + k, count)
        return d, d // members, d % members

    barrier = pltpu.get_barrier_semaphore()

    def greet(k):
        _, p, q = device(k)
        pl.semaphore_signal(barrier, inc=1, device_id={"gossip": p, "mp": q}, device_id_type=MESH)

    each(1, count, greet)

    def wide_copy(slot, ref, d, p, q, into):
        return pltpu.make_async_remote_copy(
            src_ref=ref.at[me], dst_ref=ref.at[into], send_sem=send_n.at[slot, d], recv_sem=recv_n.at[slot, into],
            device_id={"gossip": p, "mp": q}, device_id_type=MESH)

    def wide_start(slot, ref):
        def act(k):
            d, p, q = device(k)
            wide_copy(slot, ref, d, p, q, me).start()
        each(1, count, act)

    def wide_finish(slot, ref):
        def act(k):
            d, p, q = device(k)
            wide_copy(slot, ref, d, p, q, d).wait()
        each(1, count, act)

    def gossip_peers(act):
        each(1, groups, lambda k: act(lax.rem(g + k, groups)))

    def mp_peers(act):
        each(1, members, lambda k: act(lax.rem(m + k, members)))

    def pair_copy(p, into):
        return pltpu.make_async_remote_copy(
            src_ref=pairs.at[g], dst_ref=pairs.at[into], send_sem=send_t.at[phases, p], recv_sem=recv_t.at[phases, into],
            device_id={"gossip": p}, device_id_type=MESH)

    def piece_copy(h, p, into):
        return pltpu.make_async_remote_copy(
            src_ref=owned.at[h, p], dst_ref=first.at[h, into], send_sem=send_t.at[h, p], recv_sem=recv_t.at[h, into],
            device_id={"gossip": p}, device_id_type=MESH)

    def gram_copy(q, into):
        return pltpu.make_async_remote_copy(
            src_ref=grams.at[m], dst_ref=grams.at[into], send_sem=send_m.at[q], recv_sem=recv_m.at[into],
            device_id={"mp": q}, device_id_type=MESH)

    def bd_copy(h, q, into):
        return pltpu.make_async_remote_copy(
            src_ref=bd_send.at[h, q], dst_ref=bd_in.at[h, into], send_sem=send_u.at[0, h, q], recv_sem=recv_u.at[0, h, into],
            device_id={"mp": q}, device_id_type=MESH)

    def a_copy(h, q, into):
        return pltpu.make_async_remote_copy(
            src_ref=a_send.at[h, q], dst_ref=a_in.at[h, into], send_sem=send_u.at[1, h, q], recv_sem=recv_u.at[1, h, into],
            device_id={"mp": q}, device_id_type=MESH)

    def result_copy(h, k, from_device, from_p, from_q):
        d, p, q = device(k)
        return pltpu.make_async_remote_copy(
            src_ref=reply.at[h, p], dst_ref=final.at[h, from_q, from_p], send_sem=send_f.at[h, d],
            recv_sem=recv_f.at[h, from_device], device_id={"gossip": p, "mp": q}, device_id_type=MESH)

    squares[...] = jnp.zeros_like(squares)
    basis_copy.wait()
    high, low = high_low(pv[...])
    basis[...] = jnp.concatenate([high, low], axis=0)

    def fold(value):
        return value + pltpu.roll(value, rank, 1)

    def lower(value):
        return lax.broadcasted_iota(jnp.int32, value.shape, value.ndim - 1) < rank

    def place(i):
        j = i // subs
        return j // members, lax.rem(m + j % members + 1, members), pl.ds(pl.multiple_of((i % subs) * step, step), step)

    def grad_step(i):
        grad_copy(i).wait()
        weight_copy(i).start()
        products = []
        for index in range(ROUNDS):
            grad = gv[index, span(i)]
            wide = grad.astype(F32)
            squares[index] += jnp.sum((wide * wide).reshape(step // 8, 8, columns), axis=0)
            products.append(fold(dot_t(grad, basis[...])))
        h, q, inside = place(i)
        both = jnp.where(lower(products[0]), products[0], products[1])
        bd_own[h, inside] = both
        bd_send[h, q, inside] = both.astype(BF16)

    each(0, steps, grad_step)
    public_copy.start()
    partners_copy.wait()
    for index in range(ROUNDS):
        norms[me, index : index + 1] = jnp.full((1, lanes), jnp.sum(squares[index]), F32)
        pairs[g, index : index + 1] = jnp.full((1, lanes), partners_ref[index].astype(F32), F32)

    pl.semaphore_wait(barrier, count - 1)
    wide_start(0, norms)
    for h in range(phases):
        mp_peers(lambda q: bd_copy(h, q, m).start())

    parts = dot_t(basis[...], basis[...])
    folded = parts + pltpu.roll(parts, rank, 1)
    grams[m] = folded[:rank] + folded[rank:]
    mp_peers(lambda q: gram_copy(q, m).start())
    gossip_peers(lambda p: pair_copy(p, g).start())

    def weight_step(i):
        weight_copy(i).wait()
        high, low = high_low(half_ref[0, span(i)])
        product = fold(dot_t(high, basis[...]) + dot_t(low, basis[...]))
        h, q, inside = place(i)
        a_own[h, inside] = product
        packed = jnp.where(lower(product[: step // 2]), product[: step // 2], product[step // 2 :])
        a_send[h, q, i % subs] = packed.astype(BF16)

    def weight_block(j):
        each(0, subs, lambda s: weight_step(j * subs + s))

        @pl.when(j % members < members - 1)
        def _():
            a_copy(j // members, lax.rem(m + j % members + 1, members), m).start()

    each(0, phases * members, weight_block)

    mp_peers(lambda q: gram_copy(q, q).wait())
    gram = grams[0]
    for index in range(1, members):
        gram = gram + grams[index]
    gram_row = lax.broadcasted_iota(jnp.int32, gram.shape, 0)
    gram_lane = lax.broadcasted_iota(jnp.int32, gram.shape, 1)
    mixer_high, mixer_low = high_low(jnp.where(gram_lane < rank, jnp.where(gram_row == gram_lane, 1.0, 0.0) - gram, 0.0))
    public_copy.wait()
    for h in range(phases):
        at = pl.ds(pl.multiple_of((h * members + m) * block, block), block)
        high, low = high_low(cv[:, at])
        extra[h] = t_dot(high, mixer_high) + t_dot(low, mixer_high) + t_dot(high, mixer_low)

    wide_finish(0, norms)
    norm = jnp.sqrt(jnp.sum(norms[...], axis=0) / total + epsilon)
    scale = step_size * jnp.minimum(1.0, clip_limit / norm)
    scale_0 = scale[0:1]
    scale_1 = scale[1:2]

    for h in range(phases):
        def arrive(q):
            bd_copy(h, q, q).wait()
            a_copy(h, q, q).wait()
        mp_peers(arrive)
        both = bd_own[h]
        adds = [jnp.zeros((step // 2, lanes), F32) for _ in range(subs)]
        for index in range(1, members):
            q = lax.rem(m + index, members)
            both = both + bd_in[h, q].astype(F32)
            adds = [adds[s] + a_in[h, q, s].astype(F32) for s in range(subs)]
        spread = []
        for s in range(subs):
            turned = pltpu.roll(adds[s], rank, 1)
            spread.append(jnp.where(lower(turned), adds[s], turned))
            spread.append(jnp.where(lower(turned), turned, adds[s]))
        value = a_own[h] + extra[h] + jnp.concatenate(spread, axis=0)
        moved = pltpu.roll(both, rank, 1)
        value = value - jnp.where(lower(both), scale_0 * both, scale_0 * moved + scale_1 * both)
        owned[h] = value.reshape(groups, rows, lanes).astype(BF16)
        gossip_peers(lambda p: piece_copy(h, p, g).start())
        first[h, g] = owned[h, g]

    slab = min(16, step)

    def half_step(i):
        at = pl.ds(pl.multiple_of(i * slab, slab), slab)
        half_ref[0, at] = half_ref[0, at] - scale_0[0, 0] * gv[0, at].astype(F32) - scale_1[0, 0] * gv[1, at].astype(F32)

    each(0, gv.shape[1] // slab, half_step)

    gossip_peers(lambda p: pair_copy(p, p).wait())
    inside = lax.broadcasted_iota(jnp.int32, (rows, flat), 0).astype(F32)
    column = lax.broadcasted_iota(jnp.int32, (rows, flat), 1).astype(F32)
    for index in range(ROUNDS):
        blocks = []
        for replica in range(groups):
            wanted = pairs[replica, index : index + 1, 0:1] * float(rows) + inside
            blocks.append(jnp.where(wanted == column, 1.0, 0.0))
        choose[index] = jnp.concatenate(blocks, axis=0).astype(BF16)

    zeros = jnp.zeros((rank, lanes), F32)
    gram_high, gram_low = high_low(jnp.concatenate([gram, zeros], axis=0))
    unit_row = lax.broadcasted_iota(jnp.int32, (lanes, lanes), 0)
    unit_lane = lax.broadcasted_iota(jnp.int32, (lanes, lanes), 1)
    unit = jnp.where(unit_row % rank == unit_lane % rank, 1.0, 0.0).astype(BF16)

    def through(value):
        high, low = high_low(value)
        return dot(high, gram_high) + dot(low, gram_high) + dot(high, gram_low)

    for h in range(phases):
        gossip_peers(lambda p: piece_copy(h, p, p).wait())
        state = first[h].astype(F32).reshape(flat, lanes)
        narrow = state.astype(BF16)
        apart = dot(choose[0], narrow) - state
        again = (dot(narrow, unit) + through(mixing * apart - state)).astype(BF16)
        sent = again.astype(F32)
        later = dot(choose[1], again) - sent
        answer = jnp.where(lower(sent), mixing * (apart + later), sent)
        reply[h] = answer.reshape(groups, rows, lanes).astype(BF16)
        each(1, count, lambda k: result_copy(h, k, me, g, m).start())
        final[h, m, g] = reply[h, g]
        apart_ref[0, h] = jnp.where(lower(apart), apart, 0.0)
        apart_ref[1, h] = jnp.where(lower(later), later, 0.0)

    for index in range(ROUNDS):
        moved = jnp.zeros((), F32)
        for h in range(phases):
            value = apart_ref[index, h]
            moved = moved + jnp.sum(value * through(value))
        cons[me, index : index + 1] = jnp.full((1, lanes), moved, F32)
    wide_start(1, cons)
    for h in range(phases):
        def result_finish(k):
            d, p, q = device(k)
            result_copy(h, k, d, p, q).wait()
        each(1, count, result_finish)
    f_ref[...] = final[...].astype(F32).reshape(f_ref.shape)
    wide_finish(1, cons)
    stat_ref[0] = norm
    stat_ref[1] = jnp.sum(cons[...], axis=0) / total


def blend(h_ref, f_ref, b_ref, stat_ref, out_hbm, c_hbm, drift_hbm, norm_hbm,
          tiles, coefs, drift, norm, stores, others):
    rank, height = coefs.shape
    steps = stores.shape[0]
    step = height // steps

    def store(i):
        at = pl.ds(pl.multiple_of(i * step, step), step)
        return pltpu.make_async_copy(tiles.at[at], out_hbm.at[0, at], stores.at[i])

    def work(i):
        at = pl.ds(pl.multiple_of(i * step, step), step)
        part = f_ref[at, :rank].astype(BF16)
        tiles[at] = h_ref[0, at] + dot(jnp.concatenate([part, part], axis=1), b_ref[...])
        store(i).start()

    each(0, steps, work)
    for index in range(ROUNDS):
        norm[index] = jnp.max(stat_ref[0, index : index + 1, :])
        drift[index] = jnp.max(stat_ref[1, index : index + 1, :])
    coefs[...] = f_ref[...].T[rank:]
    copies = [pltpu.make_async_copy(coefs, c_hbm, others.at[0]), pltpu.make_async_copy(drift, drift_hbm, others.at[1]),
              pltpu.make_async_copy(norm, norm_hbm, others.at[2])]
    for copy in copies:
        copy.start()
    for copy in copies:
        copy.wait()
    each(0, steps, lambda i: store(i).wait())


def body(params, public, gradients, projection, partners):
    groups = lax.axis_size("gossip")
    members = lax.axis_size("mp")
    _, height, columns = params.shape
    rank = projection.shape[1]
    lanes = 2 * rank
    count = groups * members
    total = height * columns * count
    phases = 2 if height % (32 * count) == 0 else 1
    rows = height // (count * phases)
    block = height // (members * phases)
    step = min(128, block)
    subs = block // step
    steps = height // step
    flat = groups * rows
    dma = pltpu.SemaphoreType.DMA
    half, final, basis, stats = pl.pallas_call(
        functools.partial(exchange, groups, members, total),
        in_specs=[HBM] * 5,
        out_specs=[VMEM, VMEM, VMEM, VMEM],
        out_shape=[pltpu.VMEM(params.shape, F32), pltpu.VMEM((height, lanes), F32),
                   pltpu.VMEM((lanes, columns), BF16), pltpu.VMEM((2, ROUNDS, lanes), F32)],
        scratch_shapes=[
            pltpu.VMEM((ROUNDS, height, columns), BF16),
            pltpu.VMEM((rank, height), F32),
            pltpu.VMEM((rank, columns), F32),
            pltpu.SMEM((ROUNDS,), jnp.int32),
            pltpu.VMEM((ROUNDS, 8, columns), F32),
            pltpu.VMEM((phases, block, lanes), F32),
            pltpu.VMEM((phases, block, lanes), F32),
            pltpu.VMEM((phases, block, lanes), F32),
            pltpu.VMEM((phases, members, block, lanes), BF16),
            pltpu.VMEM((phases, members, block, lanes), BF16),
            pltpu.VMEM((phases, members, subs, step // 2, lanes), BF16),
            pltpu.VMEM((phases, members, subs, step // 2, lanes), BF16),
            pltpu.VMEM((members, rank, lanes), F32),
            pltpu.VMEM((count, ROUNDS, lanes), F32),
            pltpu.VMEM((groups, ROUNDS, lanes), F32),
            pltpu.VMEM((count, ROUNDS, lanes), F32),
            pltpu.VMEM((phases, groups, rows, lanes), BF16),
            pltpu.VMEM((phases, groups, rows, lanes), BF16),
            pltpu.VMEM((ROUNDS, flat, flat), BF16),
            pltpu.VMEM((ROUNDS, phases, flat, lanes), F32),
            pltpu.VMEM((phases, groups, rows, lanes), BF16),
            pltpu.VMEM((phases, members, groups, rows, lanes), BF16),
            dma((steps,)), dma((steps,)), dma((3,)),
            dma((2, count)), dma((2, count)), dma((phases + 1, groups)), dma((phases + 1, groups)),
            dma((members,)), dma((members,)), dma((2, phases, members)), dma((2, phases, members)),
            dma((phases, count)), dma((phases, count)),
        ],
        compiler_params=pltpu.CompilerParams(collective_id=0, has_side_effects=True, vmem_limit_bytes=30 << 20),
        name="exchange",
    )(*[pltpu.with_memory_space_constraint(value, pltpu.HBM) for value in
        (params, gradients, public[0].T, projection.T, partners.reshape(ROUNDS))])

    weights, coefs, drift, norm = pl.pallas_call(
        blend,
        in_specs=[VMEM, VMEM, VMEM, VMEM],
        out_specs=[ANYWHERE, ANYWHERE, ANYWHERE, ANYWHERE],
        out_shape=[jax.ShapeDtypeStruct(params.shape, F32), jax.ShapeDtypeStruct((rank, height), F32),
                   jax.ShapeDtypeStruct((ROUNDS,), F32), jax.ShapeDtypeStruct((ROUNDS,), F32)],
        scratch_shapes=[pltpu.VMEM((height, columns), F32), pltpu.VMEM((rank, height), F32),
                        pltpu.SMEM((ROUNDS,), F32), pltpu.SMEM((ROUNDS,), F32),
                        dma((height // min(128, height),)), dma((3,))],
        compiler_params=pltpu.CompilerParams(vmem_limit_bytes=20 << 20),
        name="blend",
    )(half, final, basis, stats)
    return (weights, coefs.T[None], drift, norm)


def solution(mesh):
    return jax.shard_map(
        body,
        mesh=mesh,
        in_specs=(
            P("gossip", None, "mp"),
            P("gossip", None, None),
            P(None, "gossip", None, "mp"),
            P("mp", None),
            P(None, "gossip"),
        ),
        out_specs=(P("gossip", None, "mp"), P("gossip", None, None), P(), P()),
        check_vma=False,
    )
```

time: 57.7 us -> 39 us (0.68)
  the two profiles are of different devices: /device:TPU:14 before, /device:TPU:0 now
where the time goes in v1:
time: 39 us; the launch traced here: 38.9 us
  Pallas kernels  38.2 us (98%)
  between operations  0.64 us (2%)
    pallas_call x1, Pallas kernels, body(): pl.pallas_call(functools.partial(exchange, groups, members, total), in_sp...  34.3 us
    pallas_call x1, Pallas kernels, body(): pl.pallas_call(blend, in_specs=[VMEM, VMEM, VMEM, VMEM], out_specs=[ANYWH...  3.9 us

profile of v1, /device:TPU:0, one launch (start us, length us, event | category | flops | bytes accessed | tf_op | source)
XLA Modules:
  0.0 38.9 jit_solution(172588448650822508)
XLA Ops:
  0.6 34.3 %exchange.1 = (f32[1,1024,2048]{2,1,0:T(8,128)S(1)}, f32[1024,128]{1,0:T(8,128)S(1)}, bf16[128,2048]{1,0:T(8,128)(2,1)S(1)}, f32[2,2,128]{2,1,0:T(2,128)S(1)}) custom-call(f32[1,1024,2048]{2,1,0:T(8,128)} %w_hbm.1, bf16[2,1,1024,2048]{3,2,1,0:T(8,128)(2,1)} %g_hbm.1, f32[64,1024]{1,0:T(8,128)} %bitcast.9, f32[64,2048]{1,0:T(8,128)} %bitcast.8, s32[2]{0:T(128)} %bitcast.10), custom_call_target="tpu_custom_call" | custom-call | tf_op jit(solution)/shard_map/exchange/pallas_call | solution.py:363
  35.0 3.9 %blend.1 = (f32[1,1024,2048]{2,1,0:T(8,128)}, f32[64,1024]{1,0:T(8,128)}, f32[2]{0:T(128)}, f32[2]{0:T(128)}) custom-call(f32[1,1024,2048]{2,1,0:T(8,128)S(1)} %get-tuple-element.12.h_ref, f32[1024,128]{1,0:T(8,128)S(1)} %get-tuple-element.13.f_ref, bf16[128,2048]{1,0:T(8,128)(2,1)S(1)} %get-tuple-element.14.b_ref, f32[2,2,128]{2,1,0:T(2,128)S(1)} %get-tuple-element.15.stat_ref), custom_call_target="tpu_custom_call" | custom-call | tf_op jit(solution)/shard_map/blend/pallas_call | solution.py:402

commit v2 on v1

v2 whole, which is shorter than its diff:
```python
import functools

import jax
import jax.numpy as jnp
from jax import lax
from jax.experimental import pallas as pl
from jax.experimental.pallas import tpu as pltpu
from jax.sharding import PartitionSpec as P

ROUNDS = 2
step_size = 1.0
clip_limit = 0.5
mixing = 0.4
epsilon = 1e-06

F32 = jnp.float32
BF16 = jnp.bfloat16
VMEM = pl.BlockSpec(memory_space=pltpu.VMEM)
HBM = pl.BlockSpec(memory_space=pltpu.HBM)
ANYWHERE = pl.BlockSpec(memory_space=pl.ANY)
MESH = pl.DeviceIdType.MESH


def high_low(value):
    high = value.astype(BF16)
    return high, (value - high.astype(F32)).astype(BF16)


def dot(a, b):
    return jnp.dot(a, b, preferred_element_type=F32)


def dot_t(a, b):
    return lax.dot_general(a, b, (((1,), (1,)), ((), ())), preferred_element_type=F32)


def t_dot(a, b):
    return lax.dot_general(a, b, (((0,), (0,)), ((), ())), preferred_element_type=F32)


def each(low, high, act):
    lax.fori_loop(low, high, lambda i, _: (act(i), 0)[1], 0)


def exchange(groups, members, total, w_hbm, g_hbm, c_hbm, p_hbm, partners_hbm,
             half_ref, f_ref, basis, stat_ref,
             tall, gv, cv, pv, partners_ref, squares, kept, extra, leave, land, grams,
             norms, pairs, cons, owned, first, choose, apart_ref, reply, final,
             load_g, load_w, load_p, send, recv):
    g = lax.axis_index("gossip")
    m = lax.axis_index("mp")
    count = groups * members
    me = g * members + m
    phases, block, lanes = extra.shape
    subs = land.shape[3]
    step = block // subs
    steps = phases * members * subs
    rows = owned.shape[2]
    flat = groups * rows
    rank = lanes // 2
    columns = gv.shape[2]

    def wrap(value, size):
        return jnp.where(value >= size, value - size, value)

    def place(j):
        return j % phases, wrap(m + j // phases + 1, members)

    def span(i):
        h, q = place(i // subs)
        return pl.ds(pl.multiple_of((h * members + q) * block + (i % subs) * step, step), step)

    def grad_copy(i):
        return pltpu.make_async_copy(g_hbm.at[:, 0, span(i)], gv.at[:, span(i)], load_g.at[i])

    def weight_copy(i):
        return pltpu.make_async_copy(w_hbm.at[0, span(i)], half_ref.at[0, span(i)], load_w.at[i])

    basis_copy = pltpu.make_async_copy(p_hbm, pv, load_p.at[0])
    public_copy = pltpu.make_async_copy(c_hbm, cv, load_p.at[1])
    partners_copy = pltpu.make_async_copy(partners_hbm, partners_ref, load_p.at[2])
    basis_copy.start()
    partners_copy.start()
    each(0, steps, lambda i: grad_copy(i).start())

    def partner(k):
        return jnp.bitwise_xor(g, groups - k) if groups & (groups - 1) == 0 else wrap(g + k, groups)

    unroll = next(size for size in (5, 4, 3, 2, 1) if (groups - 1) % size == 0)

    def gossip_peers(act):
        each(0, (groups - 1) // unroll, lambda j: [act(partner(1 + j * unroll + k)) for k in range(unroll)])

    def mp_peers(act):
        for turn in range(1, members):
            act(wrap(m + turn, members))

    def all_peers(act):
        gossip_peers(lambda p: [act(p, wrap(m + turn, members)) for turn in range(members)])
        mp_peers(lambda q: act(g, q))

    barrier = pltpu.get_barrier_semaphore()

    def copy(slot, source, target, **device):
        return pltpu.make_async_remote_copy(src_ref=source, dst_ref=target, send_sem=send.at[slot],
                                            recv_sem=recv.at[slot], device_id=device, device_id_type=MESH)

    def finish(slot, ref):
        copy(slot, ref, ref, gossip=wrap(g + 1, groups), mp=m).wait()

    all_peers(lambda p, q: pl.semaphore_signal(barrier, inc=1, device_id={"gossip": p, "mp": q}, device_id_type=MESH))

    NORM, CONS, PAIR, GRAM = range(4)
    FIRST, SECOND, WEIGHT, PIECE, RESULT = range(5)

    def slot(kind, h):
        return 4 + kind * phases + h

    squares[...] = jnp.zeros_like(squares)
    basis_copy.wait()
    high, low = high_low(pv[...])
    basis[...] = jnp.concatenate([high, low], axis=0)
    tall[...] = jnp.concatenate([high.astype(F32), low.astype(F32)], axis=0).T.astype(BF16)

    def fold(value):
        return value + pltpu.roll(value, rank, 1)

    def lower(value):
        return lax.broadcasted_iota(jnp.int32, value.shape, value.ndim - 1) < rank

    def pack(value):
        half = value.shape[0] // 2
        return jnp.where(lower(value[:half]), value[:half], value[half:]).astype(BF16)

    lead = steps // 2
    others = phases * (members - 1)

    def square_step(i):
        grad_copy(i).wait()

        @pl.when(i >= lead)
        def _():
            weight_copy(i - lead).start()

        for index in range(ROUNDS):
            wide = gv[index, span(i)].astype(F32)
            squares[index] += jnp.sum((wide * wide).reshape(step // 8, 8, columns), axis=0)

    def send_step(i):
        square_step(i)
        h, q = place(i // subs)
        leave[FIRST, h, q, i % subs] = pack(fold(dot(gv[0, span(i)], tall[...])))

    def keep_step(i):
        square_step(i)
        h, _ = place(i // subs)
        kept[FIRST, h, pl.ds(pl.multiple_of((i % subs) * step, step), step)] = dot(gv[0, span(i)], tall[...])

    each(0, others * subs, send_step)
    early = max(others * subs, steps * 5 // 8)
    each(others * subs, early, keep_step)
    pl.semaphore_wait(barrier, count - 1)
    for h in range(phases):
        mp_peers(lambda q: copy(slot(FIRST, h), leave.at[FIRST, h, q], land.at[FIRST, h, m], mp=q).start())
    each(early, steps, keep_step)
    each(steps - lead, steps, lambda i: weight_copy(i).start())
    public_copy.start()
    partners_copy.wait()
    for index in range(ROUNDS):
        norms[me, index : index + 1] = jnp.full((1, lanes), jnp.sum(squares[index]), F32)
        pairs[g, index : index + 1] = jnp.full((1, lanes), partners_ref[index].astype(F32), F32)

    all_peers(lambda p, q: copy(NORM, norms.at[me], norms.at[me], gossip=p, mp=q).start())

    parts = dot_t(basis[...], basis[...])
    folded = parts + pltpu.roll(parts, rank, 1)
    grams[m] = folded[:rank] + folded[rank:]
    mp_peers(lambda q: copy(GRAM, grams.at[m], grams.at[m], mp=q).start())

    def rows_of(j):
        h, q = place(j)
        return pl.ds(pl.multiple_of((h * members + q) * block, block), block)

    def value_of(kind, j):
        if kind == WEIGHT:
            each(j * subs, (j + 1) * subs, lambda i: weight_copy(i).wait())
            return half_ref[0, rows_of(j)].astype(BF16)
        return gv[kind, rows_of(j)]

    def multiply(kind, j):
        product = dot(value_of(kind, j), tall[...])
        h, q = j % phases, wrap(m + j // phases + 1, members)
        if j >= others:
            kept[kind, h] = product
        else:
            product = fold(product)
            leave[kind, h, q] = jnp.stack([pack(product[at : at + step]) for at in range(0, block, step)])
            copy(slot(kind, h), leave.at[kind, h, q], land.at[kind, h, m], mp=q).start()

    for low, high in ((0, others), (others, phases * members)):
        for j in range(low, high):
            with jax.named_scope('second'):
                multiply(SECOND, j)
        for j in range(low, high):
            with jax.named_scope('weight'):
                multiply(WEIGHT, j)
        if low == 0:
            gossip_peers(lambda p: copy(PAIR, pairs.at[g], pairs.at[g], gossip=p).start())

    finish(GRAM, grams.at[pl.ds(0, members - 1)])
    gram = grams[0]
    for index in range(1, members):
        gram = gram + grams[index]
    gram_row = lax.broadcasted_iota(jnp.int32, gram.shape, 0)
    gram_lane = lax.broadcasted_iota(jnp.int32, gram.shape, 1)
    mixer_high, mixer_low = high_low(jnp.where(gram_lane < rank, jnp.where(gram_row == gram_lane, 1.0, 0.0) - gram, 0.0))
    public_copy.wait()
    for h in range(phases):
        at = pl.ds(pl.multiple_of((h * members + m) * block, block), block)
        high, low = high_low(cv[:, at])
        extra[h] = t_dot(high, mixer_high) + t_dot(low, mixer_high) + t_dot(high, mixer_low)

    finish(NORM, norms.at[pl.ds(0, count - 1)])
    norm = jnp.sqrt(jnp.sum(norms[...], axis=0) / total + epsilon)
    scale = step_size * jnp.minimum(1.0, clip_limit / norm)
    scale_0 = scale[0:1]
    scale_1 = scale[1:2]

    for h in range(phases):
        for kind in (FIRST, SECOND, WEIGHT):
            finish(slot(kind, h), land.at[kind, h, pl.ds(0, members - 1)])
        now = kept[WEIGHT, h] - scale_0 * kept[FIRST, h]
        value = jnp.where(lower(now), extra[h] + fold(now), fold(now - scale_1 * kept[SECOND, h]))
        for turn in range(1, members):
            q = wrap(m + turn, members)
            spread = []
            for sub in range(subs):
                first_, second_, weight_ = (land[kind, h, q, sub].astype(F32) for kind in (FIRST, SECOND, WEIGHT))
                now = weight_ - scale_0 * first_
                then = now - scale_1 * second_
                spread.append(jnp.where(lower(now), now, pltpu.roll(then, rank, 1)))
                spread.append(jnp.where(lower(now), pltpu.roll(now, rank, 1), then))
            value = value + jnp.concatenate(spread, axis=0)
        owned[h] = value.reshape(groups, rows, lanes).astype(BF16)
        gossip_peers(lambda p: copy(slot(PIECE, h), owned.at[h, p], first.at[h, g], gossip=p).start())
        first[h, g] = owned[h, g]

    slab = min(16, step)

    factor_0 = scale_0[0, 0]
    factor_1 = scale_1[0, 0]

    def half_step(i):
        at = pl.ds(pl.multiple_of(i * slab, slab), slab)
        half_ref[0, at] = half_ref[0, at] - factor_0 * gv[0, at].astype(F32) - factor_1 * gv[1, at].astype(F32)

    each(0, gv.shape[1] // slab, half_step)

    finish(PAIR, pairs.at[pl.ds(0, groups - 1)])
    inside = lax.broadcasted_iota(jnp.int32, (rows, flat), 0).astype(F32)
    column = lax.broadcasted_iota(jnp.int32, (rows, flat), 1).astype(F32)
    for index in range(ROUNDS):
        blocks = []
        for replica in range(groups):
            wanted = pairs[replica, index : index + 1, 0:1] * float(rows) + inside
            blocks.append(jnp.where(wanted == column, 1.0, 0.0))
        choose[index] = jnp.concatenate(blocks, axis=0).astype(BF16)

    zeros = jnp.zeros((rank, lanes), F32)
    gram_high, gram_low = high_low(jnp.concatenate([gram, zeros], axis=0))
    unit_row = lax.broadcasted_iota(jnp.int32, (lanes, lanes), 0)
    unit_lane = lax.broadcasted_iota(jnp.int32, (lanes, lanes), 1)
    unit = jnp.where(unit_row % rank == unit_lane % rank, 1.0, 0.0).astype(BF16)

    def through(value):
        high, low = high_low(value)
        return dot(high, gram_high) + dot(low, gram_high) + dot(high, gram_low)

    for h in range(phases):
        finish(slot(PIECE, h), first.at[h, pl.ds(0, groups - 1)])
        state = first[h].astype(F32).reshape(flat, lanes)
        narrow = state.astype(BF16)
        apart = dot(choose[0], narrow) - state
        again = (dot(narrow, unit) + through(mixing * apart - state)).astype(BF16)
        sent = again.astype(F32)
        later = dot(choose[1], again) - sent
        answer = jnp.where(lower(sent), mixing * (apart + later), sent)
        reply[h] = answer.reshape(groups, rows, lanes).astype(BF16)
        all_peers(lambda p, q: copy(slot(RESULT, h), reply.at[h, p], final.at[h, m * groups + g], gossip=p, mp=q).start())
        final[h, m * groups + g] = reply[h, g]
        apart_ref[0, h] = jnp.where(lower(apart), apart, 0.0)
        apart_ref[1, h] = jnp.where(lower(later), later, 0.0)

    for index in range(ROUNDS):
        moved = jnp.zeros((), F32)
        for h in range(phases):
            value = apart_ref[index, h]
            moved = moved + jnp.sum(value * through(value))
        cons[me, index : index + 1] = jnp.full((1, lanes), moved, F32)
    all_peers(lambda p, q: copy(CONS, cons.at[me], cons.at[me], gossip=p, mp=q).start())
    for h in range(phases):
        finish(slot(RESULT, h), final.at[h, pl.ds(0, count - 1)])
    f_ref[...] = final[...].astype(F32).reshape(f_ref.shape)
    finish(CONS, cons.at[pl.ds(0, count - 1)])
    stat_ref[0] = norm
    stat_ref[1] = jnp.sum(cons[...], axis=0) / total


def blend(h_ref, f_ref, b_ref, stat_ref, out_hbm, c_hbm, drift_hbm, norm_hbm,
          tiles, coefs, drift, norm, stores, others):
    rank, height = coefs.shape
    steps = stores.shape[0]
    step = height // steps

    def store(i):
        at = pl.ds(pl.multiple_of(i * step, step), step)
        return pltpu.make_async_copy(tiles.at[at], out_hbm.at[0, at], stores.at[i])

    def work(i):
        at = pl.ds(pl.multiple_of(i * step, step), step)
        part = f_ref[at, :rank].astype(BF16)
        tiles[at] = h_ref[0, at] + dot(jnp.concatenate([part, part], axis=1), b_ref[...])
        store(i).start()

    each(0, steps, work)
    for index in range(ROUNDS):
        norm[index] = jnp.max(stat_ref[0, index : index + 1, :])
        drift[index] = jnp.max(stat_ref[1, index : index + 1, :])
    coefs[...] = f_ref[...].T[rank:]
    copies = [pltpu.make_async_copy(coefs, c_hbm, others.at[0]), pltpu.make_async_copy(drift, drift_hbm, others.at[1]),
              pltpu.make_async_copy(norm, norm_hbm, others.at[2])]
    for copy in copies:
        copy.start()
    for copy in copies:
        copy.wait()
    each(0, steps, lambda i: store(i).wait())


def body(params, public, gradients, projection, partners):
    groups = lax.axis_size("gossip")
    members = lax.axis_size("mp")
    _, height, columns = params.shape
    rank = projection.shape[1]
    lanes = 2 * rank
    count = groups * members
    total = height * columns * count
    phases = 2 if height % (32 * count) == 0 else 1
    rows = height // (count * phases)
    block = height // (members * phases)
    step = min(128, block)
    subs = block // step
    steps = height // step
    flat = groups * rows
    dma = pltpu.SemaphoreType.DMA
    half, final, basis, stats = pl.pallas_call(
        functools.partial(exchange, groups, members, total),
        in_specs=[HBM] * 5,
        out_specs=[VMEM, VMEM, VMEM, VMEM],
        out_shape=[pltpu.VMEM(params.shape, F32), pltpu.VMEM((height, lanes), F32),
                   pltpu.VMEM((lanes, columns), BF16), pltpu.VMEM((2, ROUNDS, lanes), F32)],
        scratch_shapes=[
            pltpu.VMEM((columns, lanes), BF16),
            pltpu.VMEM((ROUNDS, height, columns), BF16),
            pltpu.VMEM((rank, height), F32),
            pltpu.VMEM((rank, columns), F32),
            pltpu.SMEM((ROUNDS,), jnp.int32),
            pltpu.VMEM((ROUNDS, 8, columns), F32),
            pltpu.VMEM((3, phases, block, lanes), F32),
            pltpu.VMEM((phases, block, lanes), F32),
            pltpu.VMEM((3, phases, members, subs, step // 2, lanes), BF16),
            pltpu.VMEM((3, phases, members, subs, step // 2, lanes), BF16),
            pltpu.VMEM((members, rank, lanes), F32),
            pltpu.VMEM((count, ROUNDS, lanes), F32),
            pltpu.VMEM((groups, ROUNDS, lanes), F32),
            pltpu.VMEM((count, ROUNDS, lanes), F32),
            pltpu.VMEM((phases, groups, rows, lanes), BF16),
            pltpu.VMEM((phases, groups, rows, lanes), BF16),
            pltpu.VMEM((ROUNDS, flat, flat), BF16),
            pltpu.VMEM((ROUNDS, phases, flat, lanes), F32),
            pltpu.VMEM((phases, groups, rows, lanes), BF16),
            pltpu.VMEM((phases, count, rows, lanes), BF16),
            dma((steps,)), dma((steps,)), dma((3,)),
            dma((4 + 5 * phases,)), dma((4 + 5 * phases,)),
        ],
        compiler_params=pltpu.CompilerParams(collective_id=0, has_side_effects=True, vmem_limit_bytes=30 << 20),
        name="exchange",
    )(*[pltpu.with_memory_space_constraint(value, pltpu.HBM) for value in
        (params, gradients, public[0].T, projection.T, partners.reshape(ROUNDS))])

    weights, coefs, drift, norm = pl.pallas_call(
        blend,
        in_specs=[VMEM, VMEM, VMEM, VMEM],
        out_specs=[ANYWHERE, ANYWHERE, ANYWHERE, ANYWHERE],
        out_shape=[jax.ShapeDtypeStruct(params.shape, F32), jax.ShapeDtypeStruct((rank, height), F32),
                   jax.ShapeDtypeStruct((ROUNDS,), F32), jax.ShapeDtypeStruct((ROUNDS,), F32)],
        scratch_shapes=[pltpu.VMEM((height, columns), F32), pltpu.VMEM((rank, height), F32),
                        pltpu.SMEM((ROUNDS,), F32), pltpu.SMEM((ROUNDS,), F32),
                        dma((height // min(128, height),)), dma((3,))],
        compiler_params=pltpu.CompilerParams(vmem_limit_bytes=20 << 20),
        name="blend",
    )(half, final, basis, stats)
    return (weights, coefs.T[None], drift, norm)


def solution(mesh):
    return jax.shard_map(
        body,
        mesh=mesh,
        in_specs=(
            P("gossip", None, "mp"),
            P("gossip", None, None),
            P(None, "gossip", None, "mp"),
            P("mp", None),
            P(None, "gossip"),
        ),
        out_specs=(P("gossip", None, "mp"), P("gossip", None, None), P(), P()),
        check_vma=False,
    )
```

time: 39 us -> 33.4 us (0.86)
  Pallas kernels: 38.2 us -> 32.6 us
    pallas_call x1, Pallas kernels: 34.3 us -> 28.7 us  [body(): pl.pallas_call(functools.partial(exchange, groups, members, total), in_sp...]
where the time goes in v2:
time: 33.4 us; the launch traced here: 33.3 us
  Pallas kernels  32.6 us (98%)
  between operations  0.64 us (2%)
    pallas_call x1, Pallas kernels, body(): pl.pallas_call(functools.partial(exchange, groups, members, total), in_sp...  28.7 us
    pallas_call x1, Pallas kernels, body(): pl.pallas_call(blend, in_specs=[VMEM, VMEM, VMEM, VMEM], out_specs=[ANYWH...  3.92 us

profile of v2, /device:TPU:0, one launch (start us, length us, event | category | flops | bytes accessed | tf_op | source)
XLA Modules:
  0.0 33.3 jit_solution(11403723538847739275)
XLA Ops:
  0.6 28.7 %exchange.1 = (f32[1,1024,2048]{2,1,0:T(8,128)S(1)}, f32[1024,128]{1,0:T(8,128)S(1)}, bf16[128,2048]{1,0:T(8,128)(2,1)S(1)}, f32[2,2,128]{2,1,0:T(2,128)S(1)}) custom-call(f32[1,1024,2048]{2,1,0:T(8,128)} %w_hbm.1, bf16[2,1,1024,2048]{3,2,1,0:T(8,128)(2,1)} %g_hbm.1, f32[64,1024]{1,0:T(8,128)} %bitcast.9, f32[64,2048]{1,0:T(8,128)} %bitcast.8, s32[2]{0:T(128)} %bitcast.10), custom_call_target="tpu_custom_call" | custom-call | tf_op jit(solution)/shard_map/exchange/pallas_call | solution.py:355
  29.4 3.9 %blend.1 = (f32[1,1024,2048]{2,1,0:T(8,128)}, f32[64,1024]{1,0:T(8,128)}, f32[2]{0:T(128)}, f32[2]{0:T(128)}) custom-call(f32[1,1024,2048]{2,1,0:T(8,128)S(1)} %get-tuple-element.12.h_ref, f32[1024,128]{1,0:T(8,128)S(1)} %get-tuple-element.13.f_ref, bf16[128,2048]{1,0:T(8,128)(2,1)S(1)} %get-tuple-element.14.b_ref, f32[2,2,128]{2,1,0:T(2,128)S(1)} %get-tuple-element.15.stat_ref), custom_call_target="tpu_custom_call" | custom-call | tf_op jit(solution)/shard_map/blend/pallas_call | solution.py:390

commit v3 on v2

--- a/solution.py
+++ b/solution.py
@@ -86,10 +86,12 @@
     def partner(k):
         return jnp.bitwise_xor(g, groups - k) if groups & (groups - 1) == 0 else wrap(g + k, groups)
 
-    unroll = next(size for size in (5, 4, 3, 2, 1) if (groups - 1) % size == 0)
+    def some_peers(low, high, act):
+        unroll = next(size for size in (5, 4, 3, 2, 1) if (high - low) % size == 0)
+        each(0, (high - low) // unroll, lambda j: [act(partner(low + j * unroll + k)) for k in range(unroll)])
 
     def gossip_peers(act):
-        each(0, (groups - 1) // unroll, lambda j: [act(partner(1 + j * unroll + k)) for k in range(unroll)])
+        some_peers(1, groups, act)
 
     def mp_peers(act):
         for turn in range(1, members):
@@ -111,7 +113,7 @@
     all_peers(lambda p, q: pl.semaphore_signal(barrier, inc=1, device_id={"gossip": p, "mp": q}, device_id_type=MESH))
 
     NORM, CONS, PAIR, GRAM = range(4)
-    FIRST, SECOND, WEIGHT, PIECE, RESULT = range(5)
+    FIRST, SECOND, WEIGHT, PIECE, RESULT, FAR, RELAY = range(7)
 
     def slot(kind, h):
         return 4 + kind * phases + h
@@ -134,6 +136,7 @@
 
     lead = steps // 2
     others = phases * (members - 1)
+    relayed = phases // 2 if groups & (groups - 1) == 0 and members > 1 else 0
 
     def square_step(i):
         grad_copy(i).wait()
@@ -278,18 +281,33 @@
 
     for h in range(phases):
         finish(slot(PIECE, h), first.at[h, pl.ds(0, groups - 1)])
-        state = first[h].astype(F32).reshape(flat, lanes)
-        narrow = state.astype(BF16)
-        apart = dot(choose[0], narrow) - state
-        again = (dot(narrow, unit) + through(mixing * apart - state)).astype(BF16)
-        sent = again.astype(F32)
-        later = dot(choose[1], again) - sent
-        answer = jnp.where(lower(sent), mixing * (apart + later), sent)
+    every = range(phases)
+    state = [first[h].astype(F32).reshape(flat, lanes) for h in every]
+    narrow = [state[h].astype(BF16) for h in every]
+    apart = [dot(choose[0], narrow[h]) - state[h] for h in every]
+    again = [(dot(narrow[h], unit) + through(mixing * apart[h] - state[h])).astype(BF16) for h in every]
+    sent = [again[h].astype(F32) for h in every]
+    later = [dot(choose[1], again[h]) - sent[h] for h in every]
+    for h in every:
+        answer = jnp.where(lower(sent[h]), mixing * (apart[h] + later[h]), sent[h])
         reply[h] = answer.reshape(groups, rows, lanes).astype(BF16)
-        all_peers(lambda p, q: copy(slot(RESULT, h), reply.at[h, p], final.at[h, m * groups + g], gossip=p, mp=q).start())
+    middle = groups // 2
+    for h in every:
+        def to_all(p):
+            for turn in range(members):
+                copy(slot(RESULT, h), reply.at[h, p], final.at[h, m * groups + g], gossip=p, mp=wrap(m + turn, members)).start()
+
+        if h < relayed:
+            some_peers(1, middle + 1, lambda p: copy(
+                slot(FAR, h), reply.at[h, p], final.at[h, m * groups + g], gossip=p).start())
+            some_peers(middle + 1, groups, to_all)
+        else:
+            gossip_peers(to_all)
+        mp_peers(lambda q: copy(slot(RESULT, h), reply.at[h, g], final.at[h, m * groups + g], mp=q).start())
         final[h, m * groups + g] = reply[h, g]
-        apart_ref[0, h] = jnp.where(lower(apart), apart, 0.0)
-        apart_ref[1, h] = jnp.where(lower(later), later, 0.0)
+    for h in every:
+        apart_ref[0, h] = jnp.where(lower(apart[h]), apart[h], 0.0)
+        apart_ref[1, h] = jnp.where(lower(later[h]), later[h], 0.0)
 
     for index in range(ROUNDS):
         moved = jnp.zeros((), F32)
@@ -298,8 +316,16 @@
             moved = moved + jnp.sum(value * through(value))
         cons[me, index : index + 1] = jnp.full((1, lanes), moved, F32)
     all_peers(lambda p, q: copy(CONS, cons.at[me], cons.at[me], gossip=p, mp=q).start())
-    for h in range(phases):
-        finish(slot(RESULT, h), final.at[h, pl.ds(0, count - 1)])
+    across = pl.ds(pl.multiple_of(m * groups + jnp.where(g >= middle, 0, middle), middle), middle)
+    for h in range(relayed):
+        finish(slot(FAR, h), final.at[h, pl.ds(0, middle)])
+        mp_peers(lambda q: copy(slot(RELAY, h), final.at[h, across], final.at[h, across], mp=q).start())
+    for h in every:
+        if h < relayed:
+            finish(slot(RELAY, h), final.at[h, pl.ds(0, (members - 1) * middle)])
+            finish(slot(RESULT, h), final.at[h, pl.ds(0, members * middle - 1)])
+        else:
+            finish(slot(RESULT, h), final.at[h, pl.ds(0, count - 1)])
     f_ref[...] = final[...].astype(F32).reshape(f_ref.shape)
     finish(CONS, cons.at[pl.ds(0, count - 1)])
     stat_ref[0] = norm
@@ -380,7 +406,7 @@
             pltpu.VMEM((phases, groups, rows, lanes), BF16),
             pltpu.VMEM((phases, count, rows, lanes), BF16),
             dma((steps,)), dma((steps,)), dma((3,)),
-            dma((4 + 5 * phases,)), dma((4 + 5 * phases,)),
+            dma((4 + 7 * phases,)), dma((4 + 7 * phases,)),
         ],
         compiler_params=pltpu.CompilerParams(collective_id=0, has_side_effects=True, vmem_limit_bytes=30 << 20),
         name="exchange",

time: 33.4 us -> 32.6 us (0.976)
  Pallas kernels: 32.6 us -> 31.8 us
    pallas_call x1, Pallas kernels: 28.7 us -> 27.9 us  [body(): pl.pallas_call(functools.partial(exchange, groups, members, total), in_sp...]
where the time goes in v3:
time: 32.6 us; the launch traced here: 32.5 us
  Pallas kernels  31.8 us (98%)
  between operations  0.64 us (2%)
    pallas_call x1, Pallas kernels, body(): pl.pallas_call(functools.partial(exchange, groups, members, total), in_sp...  27.9 us
    pallas_call x1, Pallas kernels, body(): pl.pallas_call(blend, in_specs=[VMEM, VMEM, VMEM, VMEM], out_specs=[ANYWH...  3.91 us

profile of v3, /device:TPU:0, one launch (start us, length us, event | category | flops | bytes accessed | tf_op | source)
XLA Modules:
  0.0 32.5 jit_solution(3418086236669005665)
XLA Ops:
  0.6 27.9 %exchange.1 = (f32[1,1024,2048]{2,1,0:T(8,128)S(1)}, f32[1024,128]{1,0:T(8,128)S(1)}, bf16[128,2048]{1,0:T(8,128)(2,1)S(1)}, f32[2,2,128]{2,1,0:T(2,128)S(1)}) custom-call(f32[1,1024,2048]{2,1,0:T(8,128)} %w_hbm.1, bf16[2,1,1024,2048]{3,2,1,0:T(8,128)(2,1)} %g_hbm.1, f32[64,1024]{1,0:T(8,128)} %bitcast.9, f32[64,2048]{1,0:T(8,128)} %bitcast.8, s32[2]{0:T(128)} %bitcast.10), custom_call_target="tpu_custom_call" | custom-call | tf_op jit(solution)/shard_map/exchange/pallas_call | solution.py:381
  28.5 3.9 %blend.1 = (f32[1,1024,2048]{2,1,0:T(8,128)}, f32[64,1024]{1,0:T(8,128)}, f32[2]{0:T(128)}, f32[2]{0:T(128)}) custom-call(f32[1,1024,2048]{2,1,0:T(8,128)S(1)} %get-tuple-element.12.h_ref, f32[1024,128]{1,0:T(8,128)S(1)} %get-tuple-element.13.f_ref, bf16[128,2048]{1,0:T(8,128)(2,1)S(1)} %get-tuple-element.14.b_ref, f32[2,2,128]{2,1,0:T(2,128)S(1)} %get-tuple-element.15.stat_ref), custom_call_target="tpu_custom_call" | custom-call | tf_op jit(solution)/shard_map/blend/pallas_call | solution.py:416

commit v4 on v3

--- a/solution.py
+++ b/solution.py
@@ -73,8 +73,12 @@
     def grad_copy(i):
         return pltpu.make_async_copy(g_hbm.at[:, 0, span(i)], gv.at[:, span(i)], load_g.at[i])
 
-    def weight_copy(i):
-        return pltpu.make_async_copy(w_hbm.at[0, span(i)], half_ref.at[0, span(i)], load_w.at[i])
+    def rows_of(j):
+        h, q = place(j)
+        return pl.ds(pl.multiple_of((h * members + q) * block, block), block)
+
+    def weight_copy(j):
+        return pltpu.make_async_copy(w_hbm.at[0, rows_of(j)], half_ref.at[0, rows_of(j)], load_w.at[j])
 
     basis_copy = pltpu.make_async_copy(p_hbm, pv, load_p.at[0])
     public_copy = pltpu.make_async_copy(c_hbm, cv, load_p.at[1])
@@ -132,18 +136,20 @@
 
     def pack(value):
         half = value.shape[0] // 2
-        return jnp.where(lower(value[:half]), value[:half], value[half:]).astype(BF16)
-
-    lead = steps // 2
+        top, bottom = value[:half], value[half:]
+        return (jnp.where(lower(top), top, bottom) + pltpu.roll(jnp.where(lower(top), bottom, top), rank, 1)).astype(BF16)
+
+    blocks = phases * members
+    lead = blocks // 2 * subs
     others = phases * (members - 1)
     relayed = phases // 2 if groups & (groups - 1) == 0 and members > 1 else 0
 
     def square_step(i):
         grad_copy(i).wait()
 
-        @pl.when(i >= lead)
+        @pl.when((i >= lead) & (i % subs == 0))
         def _():
-            weight_copy(i - lead).start()
+            weight_copy((i - lead) // subs).start()
 
         for index in range(ROUNDS):
             wide = gv[index, span(i)].astype(F32)
@@ -152,7 +158,7 @@
     def send_step(i):
         square_step(i)
         h, q = place(i // subs)
-        leave[FIRST, h, q, i % subs] = pack(fold(dot(gv[0, span(i)], tall[...])))
+        leave[FIRST, h, q, i % subs] = pack(dot(gv[0, span(i)], tall[...]))
 
     def keep_step(i):
         square_step(i)
@@ -162,31 +168,30 @@
     each(0, others * subs, send_step)
     early = max(others * subs, steps * 5 // 8)
     each(others * subs, early, keep_step)
+    parts = dot_t(basis[...], basis[...])
+    folded = parts + pltpu.roll(parts, rank, 1)
+    full = folded[:rank] + folded[rank:]
+    grams[m] = jnp.where(lower(full[: rank // 2]), full[: rank // 2], full[rank // 2 :])
     pl.semaphore_wait(barrier, count - 1)
     for h in range(phases):
         mp_peers(lambda q: copy(slot(FIRST, h), leave.at[FIRST, h, q], land.at[FIRST, h, m], mp=q).start())
     each(early, steps, keep_step)
-    each(steps - lead, steps, lambda i: weight_copy(i).start())
+    each(blocks - blocks // 2, blocks, lambda j: weight_copy(j).start())
     public_copy.start()
     partners_copy.wait()
+    sums = []
     for index in range(ROUNDS):
-        norms[me, index : index + 1] = jnp.full((1, lanes), jnp.sum(squares[index]), F32)
+        sums.append(jnp.full((1, lanes), jnp.sum(squares[index]), F32))
         pairs[g, index : index + 1] = jnp.full((1, lanes), partners_ref[index].astype(F32), F32)
+    norms[me] = jnp.where(lower(sums[0]), sums[0], sums[1])
 
     all_peers(lambda p, q: copy(NORM, norms.at[me], norms.at[me], gossip=p, mp=q).start())
 
-    parts = dot_t(basis[...], basis[...])
-    folded = parts + pltpu.roll(parts, rank, 1)
-    grams[m] = folded[:rank] + folded[rank:]
     mp_peers(lambda q: copy(GRAM, grams.at[m], grams.at[m], mp=q).start())
-
-    def rows_of(j):
-        h, q = place(j)
-        return pl.ds(pl.multiple_of((h * members + q) * block, block), block)
 
     def value_of(kind, j):
         if kind == WEIGHT:
-            each(j * subs, (j + 1) * subs, lambda i: weight_copy(i).wait())
+            weight_copy(j).wait()
             return half_ref[0, rows_of(j)].astype(BF16)
         return gv[kind, rows_of(j)]
 
@@ -196,7 +201,6 @@
         if j >= others:
             kept[kind, h] = product
         else:
-            product = fold(product)
             leave[kind, h, q] = jnp.stack([pack(product[at : at + step]) for at in range(0, block, step)])
             copy(slot(kind, h), leave.at[kind, h, q], land.at[kind, h, m], mp=q).start()
 
@@ -211,9 +215,11 @@
             gossip_peers(lambda p: copy(PAIR, pairs.at[g], pairs.at[g], gossip=p).start())
 
     finish(GRAM, grams.at[pl.ds(0, members - 1)])
-    gram = grams[0]
+    packed = grams[0]
     for index in range(1, members):
-        gram = gram + grams[index]
+        packed = packed + grams[index]
+    turned = pltpu.roll(packed, rank, 1)
+    gram = jnp.concatenate([jnp.where(lower(packed), packed, turned), jnp.where(lower(packed), turned, packed)], axis=0)
     gram_row = lax.broadcasted_iota(jnp.int32, gram.shape, 0)
     gram_lane = lax.broadcasted_iota(jnp.int32, gram.shape, 1)
     mixer_high, mixer_low = high_low(jnp.where(gram_lane < rank, jnp.where(gram_row == gram_lane, 1.0, 0.0) - gram, 0.0))
@@ -225,6 +231,8 @@
 
     finish(NORM, norms.at[pl.ds(0, count - 1)])
     norm = jnp.sqrt(jnp.sum(norms[...], axis=0) / total + epsilon)
+    turned = pltpu.roll(norm, rank, 1)
+    norm = jnp.concatenate([jnp.where(lower(norm), norm, turned), jnp.where(lower(norm), turned, norm)], axis=0)
     scale = step_size * jnp.minimum(1.0, clip_limit / norm)
     scale_0 = scale[0:1]
     scale_1 = scale[1:2]
@@ -309,12 +317,14 @@
         apart_ref[0, h] = jnp.where(lower(apart[h]), apart[h], 0.0)
         apart_ref[1, h] = jnp.where(lower(later[h]), later[h], 0.0)
 
+    spreads = []
     for index in range(ROUNDS):
         moved = jnp.zeros((), F32)
         for h in range(phases):
             value = apart_ref[index, h]
             moved = moved + jnp.sum(value * through(value))
-        cons[me, index : index + 1] = jnp.full((1, lanes), moved, F32)
+        spreads.append(jnp.full((1, lanes), moved, F32))
+    cons[me] = jnp.where(lower(spreads[0]), spreads[0], spreads[1])
     all_peers(lambda p, q: copy(CONS, cons.at[me], cons.at[me], gossip=p, mp=q).start())
     across = pl.ds(pl.multiple_of(m * groups + jnp.where(g >= middle, 0, middle), middle), middle)
     for h in range(relayed):
@@ -329,7 +339,9 @@
     f_ref[...] = final[...].astype(F32).reshape(f_ref.shape)
     finish(CONS, cons.at[pl.ds(0, count - 1)])
     stat_ref[0] = norm
-    stat_ref[1] = jnp.sum(cons[...], axis=0) / total
+    drift = jnp.sum(cons[...], axis=0) / total
+    turned = pltpu.roll(drift, rank, 1)
+    stat_ref[1] = jnp.concatenate([jnp.where(lower(drift), drift, turned), jnp.where(lower(drift), turned, drift)], axis=0)
 
 
 def blend(h_ref, f_ref, b_ref, stat_ref, out_hbm, c_hbm, drift_hbm, norm_hbm,
@@ -395,17 +407,17 @@
             pltpu.VMEM((phases, block, lanes), F32),
             pltpu.VMEM((3, phases, members, subs, step // 2, lanes), BF16),
             pltpu.VMEM((3, phases, members, subs, step // 2, lanes), BF16),
-            pltpu.VMEM((members, rank, lanes), F32),
-            pltpu.VMEM((count, ROUNDS, lanes), F32),
+            pltpu.VMEM((members, rank // 2, lanes), F32),
+            pltpu.VMEM((count, 1, lanes), F32),
             pltpu.VMEM((groups, ROUNDS, lanes), F32),
-            pltpu.VMEM((count, ROUNDS, lanes), F32),
+            pltpu.VMEM((count, 1, lanes), F32),
             pltpu.VMEM((phases, groups, rows, lanes), BF16),
             pltpu.VMEM((phases, groups, rows, lanes), BF16),
             pltpu.VMEM((ROUNDS, flat, flat), BF16),
             pltpu.VMEM((ROUNDS, phases, flat, lanes), F32),
             pltpu.VMEM((phases, groups, rows, lanes), BF16),
             pltpu.VMEM((phases, count, rows, lanes), BF16),
-            dma((steps,)), dma((steps,)), dma((3,)),
+            dma((steps,)), dma((phases * members,)), dma((3,)),
             dma((4 + 7 * phases,)), dma((4 + 7 * phases,)),
         ],
         compiler_params=pltpu.CompilerParams(collective_id=0, has_side_effects=True, vmem_limit_bytes=30 << 20),

time: 32.6 us -> 31.7 us (0.972)
  Pallas kernels: 31.8 us -> 30.9 us
    pallas_call x1, Pallas kernels: 27.9 us -> 27 us  [body(): pl.pallas_call(functools.partial(exchange, groups, members, total), in_sp...]
where the time goes in v4:
time: 31.7 us; the launch traced here: 31.5 us
  Pallas kernels  30.9 us (97%)
  between operations  0.64 us (2%)
    pallas_call x1, Pallas kernels, body(): pl.pallas_call(functools.partial(exchange, groups, members, total), in_sp...  27 us
    pallas_call x1, Pallas kernels, body(): pl.pallas_call(blend, in_specs=[VMEM, VMEM, VMEM, VMEM], out_specs=[ANYWH...  3.9 us

profile of v4, /device:TPU:0, one launch (start us, length us, event | category | flops | bytes accessed | tf_op | source)
XLA Modules:
  0.0 31.5 jit_solution(16897789813364374899)
XLA Ops:
  0.6 27.0 %exchange.1 = (f32[1,1024,2048]{2,1,0:T(8,128)S(1)}, f32[1024,128]{1,0:T(8,128)S(1)}, bf16[128,2048]{1,0:T(8,128)(2,1)S(1)}, f32[2,2,128]{2,1,0:T(2,128)S(1)}) custom-call(f32[1,1024,2048]{2,1,0:T(8,128)} %w_hbm.1, bf16[2,1,1024,2048]{3,2,1,0:T(8,128)(2,1)} %g_hbm.1, f32[64,1024]{1,0:T(8,128)} %bitcast.9, f32[64,2048]{1,0:T(8,128)} %bitcast.8, s32[2]{0:T(128)} %bitcast.10), custom_call_target="tpu_custom_call" | custom-call | tf_op jit(solution)/shard_map/exchange/pallas_call | solution.py:393
  27.6 3.9 %blend.1 = (f32[1,1024,2048]{2,1,0:T(8,128)}, f32[64,1024]{1,0:T(8,128)}, f32[2]{0:T(128)}, f32[2]{0:T(128)}) custom-call(f32[1,1024,2048]{2,1,0:T(8,128)S(1)} %get-tuple-element.12.h_ref, f32[1024,128]{1,0:T(8,128)S(1)} %get-tuple-element.13.f_ref, bf16[128,2048]{1,0:T(8,128)(2,1)S(1)} %get-tuple-element.14.b_ref, f32[2,2,128]{2,1,0:T(2,128)S(1)} %get-tuple-element.15.stat_ref), custom_call_target="tpu_custom_call" | custom-call | tf_op jit(solution)/shard_map/blend/pallas_call | solution.py:428

commit v5 on v4

--- a/solution.py
+++ b/solution.py
@@ -302,7 +302,7 @@
     middle = groups // 2
     for h in every:
         def to_all(p):
-            for turn in range(members):
+            for turn in reversed(range(members)):
                 copy(slot(RESULT, h), reply.at[h, p], final.at[h, m * groups + g], gossip=p, mp=wrap(m + turn, members)).start()
 
         if h < relayed:

time: 31.7 us -> 31.7 us (level)
  no operation moved by 1% of the time
where the time goes in v5:
time: 31.7 us; the launch traced here: 31.5 us
  Pallas kernels  30.9 us (97%)
  between operations  0.64 us (2%)
    pallas_call x1, Pallas kernels, body(): pl.pallas_call(functools.partial(exchange, groups, members, total), in_sp...  27 us
    pallas_call x1, Pallas kernels, body(): pl.pallas_call(blend, in_specs=[VMEM, VMEM, VMEM, VMEM], out_specs=[ANYWH...  3.9 us

profile of v5, /device:TPU:0, one launch (start us, length us, event | category | flops | bytes accessed | tf_op | source)
XLA Modules:
  0.0 31.5 jit_solution(8866089065662494777)
XLA Ops:
  0.6 27.0 %exchange.1 = (f32[1,1024,2048]{2,1,0:T(8,128)S(1)}, f32[1024,128]{1,0:T(8,128)S(1)}, bf16[128,2048]{1,0:T(8,128)(2,1)S(1)}, f32[2,2,128]{2,1,0:T(2,128)S(1)}) custom-call(f32[1,1024,2048]{2,1,0:T(8,128)} %w_hbm.1, bf16[2,1,1024,2048]{3,2,1,0:T(8,128)(2,1)} %g_hbm.1, f32[64,1024]{1,0:T(8,128)} %bitcast.9, f32[64,2048]{1,0:T(8,128)} %bitcast.8, s32[2]{0:T(128)} %bitcast.10), custom_call_target="tpu_custom_call" | custom-call | tf_op jit(solution)/shard_map/exchange/pallas_call | solution.py:393
  27.6 3.9 %blend.1 = (f32[1,1024,2048]{2,1,0:T(8,128)}, f32[64,1024]{1,0:T(8,128)}, f32[2]{0:T(128)}, f32[2]{0:T(128)}) custom-call(f32[1,1024,2048]{2,1,0:T(8,128)S(1)} %get-tuple-element.12.h_ref, f32[1024,128]{1,0:T(8,128)S(1)} %get-tuple-element.13.f_ref, bf16[128,2048]{1,0:T(8,128)(2,1)S(1)} %get-tuple-element.14.b_ref, f32[2,2,128]{2,1,0:T(2,128)S(1)} %get-tuple-element.15.stat_ref), custom_call_target="tpu_custom_call" | custom-call | tf_op jit(solution)/shard_map/blend/pallas_call | solution.py:428
